TPU v7x, 32 devices: a whole 2x2x4 slice. The times are simulated.
32 devices in a mesh: eq: 2 (over x), row: 4 (over y, core), col: 4 (over z).
Axes of the slice: x: 2, y: 2, z: 4, core: 2. Of those that a mesh axis runs over, the one named last changes fastest.
Arguments:
- transition: float32 [6144, 3072], P(('eq', 'row'), 'col'), parts along dimension 0, may hold values from -0.05 to 0.9
- covariance: float32 [6144, 3072], P(('eq', 'row'), 'col'), parts along dimension 0, may hold values from -1 to 5, as said below
Outputs:
- covariance_out: float32 [6144, 3072], P(('eq', 'row'), 'col'), parts along dimension 0
- transition_out: float32 [6144, 3072], P(('eq', 'row'), 'col'), parts along dimension 0
There are 2 independent parts, one for each index of `eq`. A program takes and returns all parts, laid end to end along the dimension named above; each array names one. Nothing has to cross between parts.
Inputs may be any that keep to these rules, and one draw needn't show every extreme that they name: covariance is exactly symmetric.
All inputs are finite; a program needn't handle non-finite values.
Results may differ from a plain program's by a relative error of at most 0.0001.
Values sent between devices are 32-bit elements; how exact they have to be, the bound alone decides.
A program may use at most 128 MiB of HBM per device.

v0:
```python
import functools

import jax
import jax.numpy as jnp
from jax import lax
from jax.experimental import pallas as pl
from jax.experimental.pallas import tpu as pltpu
from jax.sharding import PartitionSpec as P

CHUNKS = 8
HALF = CHUNKS // 2
AHEAD = 2


def split(value):
    high = value.astype(jnp.bfloat16)
    return high, (value - high.astype(jnp.float32)).astype(jnp.bfloat16)


def product(stacked, high, low, transposed=False):
    dims = (((1,), (1 if transposed else 0,)), ((), ()))
    dot = functools.partial(lax.dot_general, dimension_numbers=dims, preferred_element_type=jnp.float32)
    step = stacked.shape[0] // 2
    both = dot(stacked, high)
    return both[:step] + (both[step:] + dot(stacked[:step], low))


def kernel(
    n, a_ref, x_ref, update_ref, square_ref,
    a_row, a_col, x_col, arrived, x_high, x_low, a_high, a_low, y_parts, lhs,
    local_sems, near_send, near_recv, far_send, far_recv, relay_send, relay_recv,
    gather_send, gather_recv, reduce_send, reduce_recv,
):
    r, z = lax.axis_index("row"), lax.axis_index("col")
    size = a_ref.shape[0]
    step = size // CHUNKS
    half_rows = size // 2
    last = n - 1
    pair = r // 2
    side = lax.rem(r, 2)
    far = lax.rem(r + n // 2, n)
    near = r + 1 - 2 * side
    far_near = lax.rem(near + n // 2, n)
    own_outer = jnp.where(pair == 0, 0, last)
    own_inner = jnp.where(pair == 0, 1, last - 1)
    far_outer = last - own_outer
    far_inner = last - own_inner
    at_end = (z == 0) | (z == last)
    inside = (z > 0) & (z < last)

    def rows(c):
        return pl.ds(pl.multiple_of(c * step, step), step)

    def loop(low, high, body):
        def one(i, carry):
            body(i)
            return carry

        lax.fori_loop(low, high, one, 0)

    def remote(src, dst, send, recv, **where):
        return pltpu.make_async_remote_copy(
            src_ref=src, dst_ref=dst, send_sem=send, recv_sem=recv,
            device_id=where, device_id_type=pl.DeviceIdType.MESH,
        )

    partial = x_col
    local = [
        pltpu.make_async_copy(a_ref, a_col.at[r], local_sems.at[0]),
        pltpu.make_async_copy(x_ref, x_col.at[r], local_sems.at[1]),
        pltpu.make_async_copy(x_ref, update_ref, local_sems.at[2]),
    ]
    for copy in local:
        copy.start()

    barrier = pltpu.get_barrier_semaphore()

    def greet(**where):
        pl.semaphore_signal(barrier, inc=1, device_id=where, device_id_type=pl.DeviceIdType.MESH)

    greet(row=far)
    greet(row=near)

    @pl.when(z > 0)
    def _():
        greet(col=z - 1)

    @pl.when(z < last)
    def _():
        greet(col=z + 1)

    pl.semaphore_wait(barrier, 4 - jnp.where(z == 0, 1, 0) - jnp.where(z == last, 1, 0))

    def gather_copy(right, hop, c):
        block = z - hop if right else z + hop
        slot = block if right else block - 1
        landing = a_row.at[slot, rows(c)]
        return remote(
            a_col.at[r, rows(c)] if hop == 0 else landing, landing,
            gather_send.at[0 if right else 1, hop, c], gather_recv.at[slot, c],
            col=z + 1 if right else z - 1,
        )

    def gather_arrival(block, c):
        slot = jnp.where(block > z, block - 1, block)
        remote(
            a_row.at[slot, rows(c)], a_row.at[slot, rows(c)],
            gather_send.at[0, 0, c], gather_recv.at[slot, c], row=near,
        ).wait_recv()

    def gather_own(c):
        @pl.when(z < last)
        def _():
            gather_copy(True, 0, c).start()

        @pl.when(z > 0)
        def _():
            gather_copy(False, 0, c).start()

    def pass_gather(right, hop, c):
        block = z - hop if right else z + hop
        valid = (block >= 0) if right else (block <= last)

        @pl.when(inside & valid)
        def _():
            gather_arrival(block, c)
            gather_copy(right, hop, c).start()

    def gather_slot(c):
        for hop in range(1, n - 1):
            pass_gather(True, hop, c)
            pass_gather(False, hop, c)

        @pl.when(inside & (c + AHEAD < CHUNKS))
        def _():
            gather_own(c + AHEAD)

    def gather_end(c):
        @pl.when(at_end)
        def _():
            for hop in range(1, n):
                gather_arrival(jnp.where(z == 0, hop, last - hop), c)

    def near_copy(which):
        buffer = (x_col, a_col)[which]
        return remote(buffer.at[r], buffer.at[r], near_send.at[which], near_recv.at[which], row=near)

    def near_wait(which):
        buffer = (x_col, a_col)[which]
        remote(buffer.at[near], buffer.at[near], near_send.at[which], near_recv.at[which], row=near).wait_recv()

    def half_of(piece, mine, rows_of):
        buffer = x_col if piece < 2 else a_col
        if piece < 2:
            block = (r, near)[piece] if mine else (far, far_near)[piece]
        else:
            block = ((own_outer, own_inner) if mine else (far_outer, far_inner))[piece - 2]
        return buffer.at[block, pl.ds(pl.multiple_of(rows_of * half_rows, half_rows), half_rows)]

    def far_copy(piece):
        ref = half_of(piece, True, side)
        return remote(ref, ref, far_send.at[piece], far_recv.at[piece], row=far)

    def relay_copy(piece):
        ref = half_of(piece, False, side)
        return remote(ref, ref, relay_send.at[piece], relay_recv.at[piece], row=near)

    def relay(piece):
        ref = half_of(piece, False, side)
        remote(ref, ref, far_send.at[piece], far_recv.at[piece], row=far).wait_recv()
        relay_copy(piece).start()

    def relay_wait(piece):
        ref = half_of(piece, False, 1 - side)
        remote(ref, ref, relay_send.at[piece], relay_recv.at[piece], row=near).wait_recv()

    def split_rows(which, block, low_row, count):
        source, high_ref, low_ref = ((x_col, x_high, x_low), (a_col, a_high, a_low))[which]

        def some(i):
            at = pl.multiple_of(low_row + i * step, step)
            high, low = split(source[block, pl.ds(at, step)])
            to = pl.ds(pl.multiple_of(block * size + at, step), step)
            high_ref[to] = high
            low_ref[to] = low

        loop(0, count // step, some)

    def split_half(which, block, which_half):
        split_rows(which, block, which_half * half_rows, half_rows)

    def multiply(c, high_ref, low_ref):
        for hop in range(n):
            block = lax.rem(z + hop, n)
            slot = jnp.where(block > z, block - 1, block)
            high, low = split(a_col[r, rows(c)] if hop == 0 else a_row[slot, rows(c)])
            to = pl.ds(pl.multiple_of(block * size, size), size)
            lhs[:step, to] = high
            lhs[step:, to] = low
        return product(lhs[...], high_ref[...], low_ref[...])

    def y_rows(c):
        return pl.ds(pl.multiple_of(lax.rem(c, HALF) * 2 * step, 2 * step), 2 * step)

    def compute_y(c):
        high, low = split(multiply(c, x_high, x_low))
        base = pl.multiple_of(lax.rem(c, HALF) * 2 * step, 2 * step)
        y_parts[pl.ds(base, step)] = high
        y_parts[pl.ds(pl.multiple_of(base + step, step), step)] = low

    def compute_square(c):
        square_ref[rows(c)] = multiply(c, a_high, a_low)

    def reduce_copy(right, d, c):
        target = jnp.where(right, z + 1, z - 1)
        slot = jnp.where(right & (d == target), n, d)
        return remote(
            partial.at[d, rows(c)], arrived.at[slot, rows(c)],
            reduce_send.at[d, c], reduce_recv.at[slot, c], col=target,
        )

    def reduce_wait(slot, c):
        remote(
            arrived.at[slot, rows(c)], arrived.at[slot, rows(c)],
            reduce_send.at[0, c], reduce_recv.at[slot, c], row=near,
        ).wait_recv()

    def compute_partial(c, d):
        block = pl.ds(pl.multiple_of(d * size, size), size)
        partial[d, rows(c)] = product(y_parts[y_rows(c)], a_high[block], a_low[block], transposed=True)

        @pl.when(((z == 0) & (d > 0)) | ((z == last) & (d < last)))
        def _():
            reduce_copy(z == 0, d, c).start()

    def early(c):
        gather_end(c)
        compute_y(c)
        loop(0, 2, lambda i: compute_partial(c, jnp.where(i == 0, own_outer, own_inner)))

    def late(c):
        gather_end(c)
        compute_y(c)
        loop(0, n, lambda i: compute_partial(c, jnp.where(z < n // 2, last - i, i)))

    def pass_piece(right, q):
        by_column = jnp.where(right, pair, 1 - pair) == 0
        first = q < CHUNKS
        outer = jnp.where(first & by_column, q // HALF, lax.rem(q, 2))
        c = jnp.where(first, jnp.where(by_column, lax.rem(q, HALF), q // 2), HALF + (q - CHUNKS) // 2)
        d = jnp.where(right, last - outer, outer)
        goes_on = jnp.where(right, d > z, d < z)

        @pl.when(inside & goes_on)
        def _():
            reduce_wait(d, c)
            partial[d, rows(c)] = partial[d, rows(c)] + arrived[d, rows(c)]
            reduce_copy(right, d, c).start()

    nearer_left = z < n // 2

    def first_hop(q):
        pass_piece(nearer_left, q)

    def second_hop(q):
        pass_piece(jnp.logical_not(nearer_left), q)

    local[0].wait()

    @pl.when(at_end)
    def _():
        loop(0, CHUNKS, gather_own)

    @pl.when(inside)
    def _():
        loop(0, AHEAD, gather_own)

    local[1].wait()
    far_copy(0).start()
    near_copy(0).start()
    near_copy(1).start()
    near_wait(0)
    far_copy(1).start()
    near_wait(1)
    far_copy(2).start()
    far_copy(3).start()

    def opening(c):
        gather_slot(c)

        @pl.when(c == 0)
        def _():
            split_rows(0, r, 0, size)
            split_rows(1, r, 0, size)

        @pl.when(c == 1)
        def _():
            relay(0)
            split_rows(0, near, 0, size)

        @pl.when(c == 2)
        def _():
            split_rows(1, near, 0, size)
            relay_wait(0)
            split_half(0, far, side)
            split_half(0, far_near, 1 - side)

    loop(0, HALF, opening)
    relay(1)
    split_half(0, far_near, side)
    relay_wait(1)
    split_half(0, far, 1 - side)
    near_copy(0).wait_send()
    for piece in range(2):
        far_copy(piece).wait_send()
        relay_copy(piece).wait_send()

    def second(c):
        gather_slot(HALF + c)
        early(c)

    loop(0, HALF - 1, second)
    relay(2)
    split_half(1, far_outer, side)
    relay_wait(2)
    split_half(1, far_outer, 1 - side)
    loop(0, HALF - 1, lambda c: compute_partial(c, far_outer))
    gather_slot(CHUNKS - 1)
    first_hop(0)
    first_hop(1)
    early(HALF - 1)
    compute_partial(HALF - 1, far_outer)
    first_hop(2)
    first_hop(3)
    relay(3)
    split_half(1, far_inner, side)
    relay_wait(3)
    split_half(1, far_inner, 1 - side)
    loop(0, HALF, lambda c: compute_partial(c, far_inner))

    def closing(j):
        for i in range(2):
            q = 4 + 2 * j + i

            @pl.when(q < 2 * CHUNKS)
            def _():
                first_hop(q)

        for i in range(2):
            second_hop(2 * j + i)

        @pl.when(j < HALF)
        def _():
            late(HALF + j)

        @pl.when((j >= 1) & (j <= HALF))
        def _():
            loop(2 * (j - 1), 2 * j, compute_square)

    loop(0, CHUNKS, closing)

    def finish(c):
        update_ref[rows(c)] = update_ref[rows(c)] + partial[z, rows(c)]

        @pl.when(z < last)
        def _():
            reduce_wait(z, c)
            update_ref[rows(c)] = update_ref[rows(c)] + arrived[z, rows(c)]

        @pl.when(z > 0)
        def _():
            reduce_wait(n, c)
            update_ref[rows(c)] = update_ref[rows(c)] + arrived[n, rows(c)]

    local[2].wait()
    loop(0, CHUNKS, finish)

    near_copy(1).wait_send()
    for piece in range(2, 4):
        far_copy(piece).wait_send()
        relay_copy(piece).wait_send()

    def sent(c):
        for hop in range(n - 1):
            @pl.when((z < last) & (z - hop >= 0))
            def _():
                gather_copy(True, hop, c).wait_send()

            @pl.when((z > 0) & (z + hop <= last))
            def _():
                gather_copy(False, hop, c).wait_send()

        for d in range(n):
            @pl.when(z != d)
            def _():
                reduce_copy(z < d, d, c).wait_send()

    loop(0, CHUNKS, sent)


def per_device(n, transition, covariance):
    size = transition.shape[0]
    f32, bf16 = jnp.float32, jnp.bfloat16
    shape = jax.ShapeDtypeStruct(transition.shape, f32)
    return pl.pallas_call(
        functools.partial(kernel, n),
        out_shape=(shape, shape),
        in_specs=[pl.BlockSpec(memory_space=pl.ANY)] * 2,
        out_specs=(pl.BlockSpec(memory_space=pltpu.VMEM),) * 2,
        scratch_shapes=[
            pltpu.VMEM((n - 1, size, size), f32),
            pltpu.VMEM((n, size, size), f32),
            pltpu.VMEM((n, size, size), f32),
            pltpu.VMEM((n + 1, size, size), f32),
            pltpu.VMEM((n * size, size), bf16),
            pltpu.VMEM((n * size, size), bf16),
            pltpu.VMEM((n * size, size), bf16),
            pltpu.VMEM((n * size, size), bf16),
            pltpu.VMEM((size, size), bf16),
            pltpu.VMEM((2 * size // CHUNKS, n * size), bf16),
            pltpu.SemaphoreType.DMA((3,)),
            pltpu.SemaphoreType.DMA((2,)),
            pltpu.SemaphoreType.DMA((2,)),
            pltpu.SemaphoreType.DMA((4,)),
            pltpu.SemaphoreType.DMA((4,)),
            pltpu.SemaphoreType.DMA((4,)),
            pltpu.SemaphoreType.DMA((4,)),
            pltpu.SemaphoreType.DMA((2, n - 1, CHUNKS)),
            pltpu.SemaphoreType.DMA((n - 1, CHUNKS)),
            pltpu.SemaphoreType.DMA((n, CHUNKS)),
            pltpu.SemaphoreType.DMA((n + 1, CHUNKS)),
        ],
        compiler_params=pltpu.CompilerParams(
            collective_id=0, has_side_effects=True, vmem_limit_bytes=67043328
        ),
    )(transition, covariance)


def solution(mesh):
    n = mesh.shape["col"]
    assert mesh.shape["row"] == n == 4
    spec = P(("eq", "row"), "col")
    return jax.shard_map(
        functools.partial(per_device, n),
        mesh=mesh,
        in_specs=(spec, spec),
        out_specs=(spec, spec),
        check_vma=False,
    )
```

profile of v0, /device:TPU:0, one launch (start us, length us, event | category | flops | bytes accessed | tf_op | source)
XLA Modules:
  0.0 240.8 jit_solution(5651630431178198603)
XLA Ops:
  0.6 235.4 %shard_map.41 = (f32[768,768]{1,0:T(8,128)}, f32[768,768]{1,0:T(8,128)}) custom-call(f32[768,768]{1,0:T(8,128)} %a_ref.1, f32[768,768]{1,0:T(8,128)} %x_ref.1), custom_call_target="tpu_custom_call" | custom-call | tf_op jit(solution)/shard_map/pallas_call | solution.py:405
  236.0 0.0 copy-start
  236.0 3.4 %copy.6 = f32[768,768]{1,0:T(8,128)} copy(f32[768,768]{1,0:T(8,128)} %get-tuple-element.4) | data formatting | bytes 4718592
  239.4 0.0 copy-done
  239.4 1.4 copy.7
Async XLA Ops:
  236.0 3.4 %copy-start = (f32[768,768]{1,0:T(8,128)S(1)}, f32[768,768]{1,0:T(8,128)}, u32[]{:S(2)}) copy-start(f32[768,768]{1,0:T(8,128)} %get-tuple-element.5) | copy-start | bytes 7077892
where the time goes:
time: 243 us; the launch traced here: 241 us
  Pallas kernels  235 us (97%)
  local copies, waits for them, and re-layouts  4.78 us (2%)
    pallas_call x1, Pallas kernels, per_device(): pl.pallas_call(functools.partial(kernel, n), out_shape=(shape, shape), in...  235 us

commit v1 on v0

--- a/solution.py
+++ b/solution.py
@@ -8,8 +8,33 @@
 from jax.sharding import PartitionSpec as P
 
 CHUNKS = 8
-HALF = CHUNKS // 2
 AHEAD = 2
+ORDERS = (
+  (
+    253789560, 33963514, 38176921, 245107104, 42500513, 44483107, 24132337, 154166277,
+    155554370, 157388355, 26486340, 173296626, 79196278, 211349767, 145189459, 28190437,
+    241802453, 187608183, 194440478, 30514653, 127119206, 65803222, 167244743, 219535503,
+    223122537, 227333355, 231544173, 111861487, 113991468, 99475374,
+  ),
+  (
+    253789560, 33963514, 38176921, 245107104, 42500513, 44483107, 24132337, 137768965,
+    187011681, 60207426, 192471430, 144477068, 78799990, 210953479, 117925468, 28799685,
+    120170160, 171195379, 215062686, 121874270, 179644882, 65835990, 200926139, 183289807,
+    126498024, 109737450, 128628460, 111867886, 113991468, 99473215,
+  ),
+  (
+    259964152, 247233136, 170944576, 154282306, 175940042, 205011787, 210842082, 186513868,
+    194440537, 163017413, 165131078, 219673543, 228259177, 167507821, 183872212, 268435455,
+    268435455, 268435455, 268435455, 268435455, 268435455, 268435455, 268435455, 268435455,
+    268435455, 268435455, 268435455, 268435455, 268435455, 268435455,
+  ),
+  (
+    259964152, 247233136, 137769024, 206613729, 209494490, 154286939, 210838986, 251455068,
+    196700229, 215245645, 173139806, 221917159, 230372842, 167504366, 183872212, 268435455,
+    268435455, 268435455, 268435455, 268435455, 268435455, 268435455, 268435455, 268435455,
+    268435455, 268435455, 268435455, 268435455, 268435455, 268435455,
+  ),
+)
 
 
 def split(value):
@@ -91,15 +116,20 @@
 
     pl.semaphore_wait(barrier, 4 - jnp.where(z == 0, 1, 0) - jnp.where(z == last, 1, 0))
 
-    def gather_copy(right, hop, c):
-        block = z - hop if right else z + hop
-        slot = block if right else block - 1
+    def gather_copy(right, block, c):
+        slot = jnp.where(right, block, block - 1)
         landing = a_row.at[slot, rows(c)]
-        return remote(
-            a_col.at[r, rows(c)] if hop == 0 else landing, landing,
-            gather_send.at[0 if right else 1, hop, c], gather_recv.at[slot, c],
-            col=z + 1 if right else z - 1,
-        )
+        sems = gather_send.at[jnp.where(right, 0, 1), jnp.abs(block - z), c], gather_recv.at[slot, c]
+        to = jnp.where(right, z + 1, z - 1)
+        return landing, sems, to
+
+    def gather_own(right, c):
+        landing, sems, to = gather_copy(right, z, c)
+        return remote(a_col.at[r, rows(c)], landing, *sems, col=to)
+
+    def gather_pass(right, block, c):
+        landing, sems, to = gather_copy(right, block, c)
+        return remote(landing, landing, *sems, col=to)
 
     def gather_arrival(block, c):
         slot = jnp.where(block > z, block - 1, block)
@@ -108,32 +138,18 @@
             gather_send.at[0, 0, c], gather_recv.at[slot, c], row=near,
         ).wait_recv()
 
-    def gather_own(c):
+    def own_both(c):
         @pl.when(z < last)
         def _():
-            gather_copy(True, 0, c).start()
+            gather_own(True, c).start()
 
         @pl.when(z > 0)
         def _():
-            gather_copy(False, 0, c).start()
-
-    def pass_gather(right, hop, c):
-        block = z - hop if right else z + hop
-        valid = (block >= 0) if right else (block <= last)
-
-        @pl.when(inside & valid)
-        def _():
-            gather_arrival(block, c)
-            gather_copy(right, hop, c).start()
-
-    def gather_slot(c):
-        for hop in range(1, n - 1):
-            pass_gather(True, hop, c)
-            pass_gather(False, hop, c)
-
-        @pl.when(inside & (c + AHEAD < CHUNKS))
-        def _():
-            gather_own(c + AHEAD)
+            gather_own(False, c).start()
+
+    def pass_gather(block, c):
+        gather_arrival(block, c)
+        gather_pass(block < z, block, c).start()
 
     def gather_end(c):
         @pl.when(at_end)
@@ -200,11 +216,11 @@
         return product(lhs[...], high_ref[...], low_ref[...])
 
     def y_rows(c):
-        return pl.ds(pl.multiple_of(lax.rem(c, HALF) * 2 * step, 2 * step), 2 * step)
+        return pl.ds(pl.multiple_of(c * 2 * step, 2 * step), 2 * step)
 
     def compute_y(c):
         high, low = split(multiply(c, x_high, x_low))
-        base = pl.multiple_of(lax.rem(c, HALF) * 2 * step, 2 * step)
+        base = pl.multiple_of(c * 2 * step, 2 * step)
         y_parts[pl.ds(base, step)] = high
         y_parts[pl.ds(pl.multiple_of(base + step, step), step)] = low
 
@@ -233,47 +249,71 @@
         def _():
             reduce_copy(z == 0, d, c).start()
 
-    def early(c):
-        gather_end(c)
-        compute_y(c)
-        loop(0, 2, lambda i: compute_partial(c, jnp.where(i == 0, own_outer, own_inner)))
-
-    def late(c):
-        gather_end(c)
-        compute_y(c)
-        loop(0, n, lambda i: compute_partial(c, jnp.where(z < n // 2, last - i, i)))
-
-    def pass_piece(right, q):
-        by_column = jnp.where(right, pair, 1 - pair) == 0
-        first = q < CHUNKS
-        outer = jnp.where(first & by_column, q // HALF, lax.rem(q, 2))
-        c = jnp.where(first, jnp.where(by_column, lax.rem(q, HALF), q // 2), HALF + (q - CHUNKS) // 2)
-        d = jnp.where(right, last - outer, outer)
-        goes_on = jnp.where(right, d > z, d < z)
-
-        @pl.when(inside & goes_on)
-        def _():
-            reduce_wait(d, c)
-            partial[d, rows(c)] = partial[d, rows(c)] + arrived[d, rows(c)]
-            reduce_copy(right, d, c).start()
-
-    nearer_left = z < n // 2
-
-    def first_hop(q):
-        pass_piece(nearer_left, q)
-
-    def second_hop(q):
-        pass_piece(jnp.logical_not(nearer_left), q)
+    def pass_piece(d, c):
+        reduce_wait(d, c)
+        partial[d, rows(c)] = partial[d, rows(c)] + arrived[d, rows(c)]
+        reduce_copy(d > z, d, c).start()
+
+    def landed(piece):
+        relay_wait(piece)
+        if piece < 2:
+            split_half(0, (far, far_near)[piece], side)
+            split_half(0, (far_near, far)[piece], 1 - side)
+        else:
+            split_rows(1, (far_outer, far_inner)[piece - 2], 0, size)
+        if piece == 1:
+            near_copy(0).wait_send()
+            for sent_piece in range(2):
+                far_copy(sent_piece).wait_send()
+                relay_copy(sent_piece).wait_send()
+
+    mirrored = z >= n // 2
+
+    def facing(index):
+        return jnp.where(mirrored, last - index, index)
+
+    def other(index):
+        return facing(jnp.where(index >= 1, index + 1, index))
+
+    def act(code):
+        def when(low, count, body):
+            @pl.when((code >= low) & (code < low + count))
+            def _():
+                body((code - low) // CHUNKS, lax.rem(code - low, CHUNKS))
+
+        def once(value, body):
+            @pl.when(code == value)
+            def _():
+                body()
+
+        when(0, 2 * CHUNKS, lambda i, c: gather_own((i == 0) != mirrored, c).start())
+        when(16, 3 * CHUNKS, lambda i, c: pass_gather(other(i), c))
+        when(40, 3 * CHUNKS, lambda i, c: pass_piece(other(i), c))
+
+        def begin(i, c):
+            gather_end(c)
+            compute_y(c)
+
+        when(64, CHUNKS, begin)
+        when(72, 4 * CHUNKS, lambda i, c: compute_partial(c, facing(i)))
+        when(104, CHUNKS, lambda i, c: compute_square(c))
+        for piece in range(4):
+            once(112 + piece, functools.partial(relay, piece))
+            once(116 + piece, functools.partial(landed, piece))
+        once(120, lambda: split_rows(0, r, 0, size))
+        once(121, lambda: split_rows(0, near, 0, size))
+        once(122, lambda: split_rows(1, r, 0, size))
+        once(123, lambda: split_rows(1, near, 0, size))
 
     local[0].wait()
 
     @pl.when(at_end)
     def _():
-        loop(0, CHUNKS, gather_own)
+        loop(0, CHUNKS, own_both)
 
     @pl.when(inside)
     def _():
-        loop(0, AHEAD, gather_own)
+        loop(0, AHEAD, own_both)
 
     local[1].wait()
     far_copy(0).start()
@@ -285,79 +325,24 @@
     far_copy(2).start()
     far_copy(3).start()
 
-    def opening(c):
-        gather_slot(c)
-
-        @pl.when(c == 0)
-        def _():
-            split_rows(0, r, 0, size)
-            split_rows(1, r, 0, size)
-
-        @pl.when(c == 1)
-        def _():
-            relay(0)
-            split_rows(0, near, 0, size)
-
-        @pl.when(c == 2)
-        def _():
-            split_rows(1, near, 0, size)
-            relay_wait(0)
-            split_half(0, far, side)
-            split_half(0, far_near, 1 - side)
-
-    loop(0, HALF, opening)
-    relay(1)
-    split_half(0, far_near, side)
-    relay_wait(1)
-    split_half(0, far, 1 - side)
-    near_copy(0).wait_send()
-    for piece in range(2):
-        far_copy(piece).wait_send()
-        relay_copy(piece).wait_send()
-
-    def second(c):
-        gather_slot(HALF + c)
-        early(c)
-
-    loop(0, HALF - 1, second)
-    relay(2)
-    split_half(1, far_outer, side)
-    relay_wait(2)
-    split_half(1, far_outer, 1 - side)
-    loop(0, HALF - 1, lambda c: compute_partial(c, far_outer))
-    gather_slot(CHUNKS - 1)
-    first_hop(0)
-    first_hop(1)
-    early(HALF - 1)
-    compute_partial(HALF - 1, far_outer)
-    first_hop(2)
-    first_hop(3)
-    relay(3)
-    split_half(1, far_inner, side)
-    relay_wait(3)
-    split_half(1, far_inner, 1 - side)
-    loop(0, HALF, lambda c: compute_partial(c, far_inner))
-
-    def closing(j):
-        for i in range(2):
-            q = 4 + 2 * j + i
-
-            @pl.when(q < 2 * CHUNKS)
-            def _():
-                first_hop(q)
-
-        for i in range(2):
-            second_hop(2 * j + i)
-
-        @pl.when(j < HALF)
-        def _():
-            late(HALF + j)
-
-        @pl.when((j >= 1) & (j <= HALF))
-        def _():
-            loop(2 * (j - 1), 2 * j, compute_square)
-
-    loop(0, CHUNKS, closing)
+    second = (pair == 0) == mirrored
+    choice = jnp.where(at_end, 2, 0) + jnp.where(second, 1, 0)
+
+    def four(i):
+        word = 0
+        for at in range(len(ORDERS[0])):
+            value = ORDERS[3][at]
+            for v in range(3):
+                value = jnp.where(choice == v, ORDERS[v][at], value)
+            word = jnp.where(i == at, value, word)
+
+        def one(j, left):
+            act(lax.rem(left, 128))
+            return left // 128
+
+        lax.fori_loop(0, 4, one, word)
+
+    loop(0, len(ORDERS[0]), four)
 
     def finish(c):
         update_ref[rows(c)] = update_ref[rows(c)] + partial[z, rows(c)]
@@ -384,11 +369,11 @@
         for hop in range(n - 1):
             @pl.when((z < last) & (z - hop >= 0))
             def _():
-                gather_copy(True, hop, c).wait_send()
+                gather_pass(True, z - hop, c).wait_send()
 
             @pl.when((z > 0) & (z + hop <= last))
             def _():
-                gather_copy(False, hop, c).wait_send()
+                gather_pass(False, z + hop, c).wait_send()
 
         for d in range(n):
             @pl.when(z != d)
@@ -416,7 +401,7 @@
             pltpu.VMEM((n * size, size), bf16),
             pltpu.VMEM((n * size, size), bf16),
             pltpu.VMEM((n * size, size), bf16),
-            pltpu.VMEM((size, size), bf16),
+            pltpu.VMEM((2 * size, size), bf16),
             pltpu.VMEM((2 * size // CHUNKS, n * size), bf16),
             pltpu.SemaphoreType.DMA((3,)),
             pltpu.SemaphoreType.DMA((2,)),

time: 243 us -> 226 us (0.930)
  Pallas kernels: 235 us -> 220 us
    pallas_call x1, Pallas kernels: 235 us -> 220 us  [per_device(): pl.pallas_call(functools.partial(kernel, n), out_shape=(shape, shape), in...]
where the time goes in v1:
time: 226 us
  Pallas kernels  220 us (97%)
  local copies, waits for them, and re-layouts  4.78 us (2%)
    pallas_call x1, Pallas kernels, per_device(): pl.pallas_call(functools.partial(kernel, n), out_shape=(shape, shape), in...  220 us
    unnamed x4, local copies, waits for them, and re-layouts  4.78 us

profile of v1, /device:TPU:0, one launch (start us, length us, event | category | flops | bytes accessed | tf_op | source)
XLA Modules:
  0.0 225.9 jit_solution(15052037282245544531)
XLA Ops:
  0.6 220.4 %shard_map.41 = (f32[768,768]{1,0:T(8,128)}, f32[768,768]{1,0:T(8,128)}) custom-call(f32[768,768]{1,0:T(8,128)} %a_ref.1, f32[768,768]{1,0:T(8,128)} %x_ref.1), custom_call_target="tpu_custom_call" | custom-call | tf_op jit(solution)/shard_map/pallas_call | solution.py:390
  221.1 0.0 copy-start
  221.1 3.4 %copy.6 = f32[768,768]{1,0:T(8,128)} copy(f32[768,768]{1,0:T(8,128)} %get-tuple-element.4) | data formatting | bytes 4718592
  224.5 0.0 copy-done
  224.5 1.4 copy.7
Async XLA Ops:
  221.1 3.4 %copy-start = (f32[768,768]{1,0:T(8,128)S(1)}, f32[768,768]{1,0:T(8,128)}, u32[]{:S(2)}) copy-start(f32[768,768]{1,0:T(8,128)} %get-tuple-element.5) | copy-start | bytes 7077892

commit v2 on v1

--- a/solution.py
+++ b/solution.py
@@ -9,28 +9,29 @@
 
 CHUNKS = 8
 AHEAD = 2
+LATE = 1
 ORDERS = (
   (
-    253789560, 33963514, 38176921, 245107104, 42500513, 44483107, 24132337, 154166277,
-    155554370, 157388355, 26486340, 173296626, 79196278, 211349767, 145189459, 28190437,
-    241802453, 187608183, 194440478, 30514653, 127119206, 65803222, 167244743, 219535503,
-    223122537, 227333355, 231544173, 111861487, 113991468, 99475374,
+    255721738, 6686731, 38176921, 40303216, 8931872, 247220898, 152044195, 153457217,
+    13051202, 26289603, 240395799, 15296849, 207122550, 146345699, 174286565, 81095224,
+    64879033, 190209368, 196544347, 83469115, 181348190, 256648095, 32763879, 221911255,
+    225228072, 229439017, 233649962, 111877803, 258842413, 100630318,
   ),
   (
-    253789560, 33963514, 38176921, 245107104, 42500513, 44483107, 24132337, 137768965,
-    187011681, 60207426, 192471430, 144477068, 78799990, 210953479, 117925468, 28799685,
-    120170160, 171195379, 215062686, 121874270, 179644882, 65835990, 200926139, 183289807,
-    126498024, 109737450, 128628460, 111867886, 113991468, 99473215,
+    255721738, 6686731, 38176921, 40303216, 8931872, 247220898, 202375843, 136680024,
+    59813089, 141996294, 192465804, 15295090, 156394614, 210636491, 28403292, 163017392,
+    251452582, 171186334, 214861638, 175417182, 179640615, 149868502, 167244794, 219535759,
+    223286377, 227349739, 231691629, 93148655, 258693950, 100630318,
   ),
   (
-    259964152, 247233136, 170944576, 154282306, 175940042, 205011787, 210842082, 186513868,
-    194440537, 163017413, 165131078, 219673543, 228259177, 167507821, 183872212, 268435455,
+    245120248, 168835825, 154427592, 141732162, 248703474, 209236192, 242430532, 190213239,
+    212954715, 215066333, 219277150, 228259177, 177993581, 267758287, 268435455, 268435455,
     268435455, 268435455, 268435455, 268435455, 268435455, 268435455, 268435455, 268435455,
     268435455, 268435455, 268435455, 268435455, 268435455, 268435455,
   ),
   (
-    259964152, 247233136, 137769024, 206613729, 209494490, 154286939, 210838986, 251455068,
-    196700229, 215245645, 173139806, 221917159, 230372842, 167504366, 183872212, 268435455,
+    245120248, 202390257, 188244184, 141996354, 248967666, 158508232, 160903748, 212958195,
+    148121309, 171159398, 224031815, 175846866, 234174317, 267758287, 268435455, 268435455,
     268435455, 268435455, 268435455, 268435455, 268435455, 268435455, 268435455, 268435455,
     268435455, 268435455, 268435455, 268435455, 268435455, 268435455,
   ),
@@ -54,7 +55,7 @@
     n, a_ref, x_ref, update_ref, square_ref,
     a_row, a_col, x_col, arrived, x_high, x_low, a_high, a_low, y_parts, lhs,
     local_sems, near_send, near_recv, far_send, far_recv, relay_send, relay_recv,
-    gather_send, gather_recv, reduce_send, reduce_recv,
+    gather_send, gather_recv, reduce_send, reduce_recv, end_send, end_recv, free_sems,
 ):
     r, z = lax.axis_index("row"), lax.axis_index("col")
     size = a_ref.shape[0]
@@ -72,6 +73,7 @@
     far_inner = last - own_inner
     at_end = (z == 0) | (z == last)
     inside = (z > 0) & (z < last)
+    beside = jnp.where(z == 0, 1, last - 1)
 
     def rows(c):
         return pl.ds(pl.multiple_of(c * step, step), step)
@@ -190,20 +192,21 @@
         ref = half_of(piece, False, 1 - side)
         remote(ref, ref, relay_send.at[piece], relay_recv.at[piece], row=near).wait_recv()
 
-    def split_rows(which, block, low_row, count):
-        source, high_ref, low_ref = ((x_col, x_high, x_low), (a_col, a_high, a_low))[which]
-
+    x_pair, a_pair = (x_high, x_low), (a_high, a_low)
+
+    def split_rows(source, pair_refs, block, low_row, count):
         def some(i):
             at = pl.multiple_of(low_row + i * step, step)
-            high, low = split(source[block, pl.ds(at, step)])
             to = pl.ds(pl.multiple_of(block * size + at, step), step)
-            high_ref[to] = high
-            low_ref[to] = low
+            pair_refs[0][to], pair_refs[1][to] = split(source[pl.ds(at, step)])
 
         loop(0, count // step, some)
 
-    def split_half(which, block, which_half):
-        split_rows(which, block, which_half * half_rows, half_rows)
+    def split_half(block, which_half):
+        split_rows(x_col.at[block], x_pair, block, which_half * half_rows, half_rows)
+
+    def split_all(source, pair_refs, block):
+        split_rows(source, pair_refs, block, 0, size)
 
     def multiply(c, high_ref, low_ref):
         for hop in range(n):
@@ -219,7 +222,13 @@
         return pl.ds(pl.multiple_of(c * 2 * step, 2 * step), 2 * step)
 
     def compute_y(c):
-        high, low = split(multiply(c, x_high, x_low))
+        value = multiply(c, x_high, x_low)
+
+        @pl.when(at_end & (c >= CHUNKS - LATE))
+        def _():
+            partial[beside, rows(c)] = value
+
+        high, low = split(value)
         base = pl.multiple_of(c * 2 * step, 2 * step)
         y_parts[pl.ds(base, step)] = high
         y_parts[pl.ds(pl.multiple_of(base + step, step), step)] = low
@@ -257,17 +266,78 @@
     def landed(piece):
         relay_wait(piece)
         if piece < 2:
-            split_half(0, (far, far_near)[piece], side)
-            split_half(0, (far_near, far)[piece], 1 - side)
+            split_half((far, far_near)[piece], side)
+            split_half((far_near, far)[piece], 1 - side)
         else:
-            split_rows(1, (far_outer, far_inner)[piece - 2], 0, size)
+            block = (far_outer, far_inner)[piece - 2]
+            split_all(a_col.at[block], a_pair, block)
         if piece == 1:
             near_copy(0).wait_send()
             for sent_piece in range(2):
                 far_copy(sent_piece).wait_send()
                 relay_copy(sent_piece).wait_send()
+        if piece == 3:
+            for sent_piece in range(2, 4):
+                far_copy(sent_piece).wait_send()
+                relay_copy(sent_piece).wait_send()
+
+            @pl.when(inside)
+            def _():
+                for at, row in ((0, near), (1, far)):
+                    pl.semaphore_signal(
+                        free_sems.at[at], inc=1, device_id={"row": row}, device_id_type=pl.DeviceIdType.MESH
+                    )
 
     mirrored = z >= n // 2
+    end_slot = jnp.where(mirrored, n - 2, 0)
+
+    def end_copy(which):
+        source, block, row = (
+            (a_row.at[end_slot], r, far), (a_row.at[end_slot], r, near), (a_col.at[far], far, near)
+        )[which]
+        return remote(source, a_col.at[block], end_send.at[which], end_recv.at[which], row=row)
+
+    def end_wait(which):
+        block = (far, near, far_near)[which]
+        remote(a_col.at[block], a_col.at[block], end_send.at[which], end_recv.at[which], row=near).wait_recv()
+
+    def end_start():
+        pl.semaphore_wait(free_sems.at[0], 1)
+        pl.semaphore_wait(free_sems.at[1], 1)
+        end_copy(0).start()
+        end_copy(1).start()
+
+    def end_middle():
+        end_wait(0)
+        end_copy(2).start()
+        split_all(a_row.at[end_slot], x_pair, r)
+        end_wait(1)
+        split_all(a_col.at[near], x_pair, near)
+        split_all(a_col.at[far], x_pair, far)
+
+    def end_last():
+        end_wait(2)
+        split_all(a_col.at[far_near], x_pair, far_near)
+
+    def end_partials(c):
+        slot = jnp.where(mirrored, z, n)
+        reduce_wait(slot, c)
+        high, low = split(arrived[slot, rows(c)])
+        lhs[:step, :size] = high
+        lhs[step:, :size] = low
+
+        def one(i):
+            d = jnp.where(mirrored, i, last - i)
+            block = pl.ds(pl.multiple_of(d * size, size), size)
+            partial[d, rows(c)] = partial[d, rows(c)] + product(
+                lhs[:, :size], x_high[block], x_low[block], transposed=True
+            )
+
+            @pl.when(i < n // 2)
+            def _():
+                reduce_copy(d > z, d, c).start()
+
+        loop(0, n - 1, one)
 
     def facing(index):
         return jnp.where(mirrored, last - index, index)
@@ -293,6 +363,10 @@
         def begin(i, c):
             gather_end(c)
             compute_y(c)
+
+            @pl.when(at_end & (c >= CHUNKS - LATE))
+            def _():
+                reduce_copy(z == 0, beside, c).start()
 
         when(64, CHUNKS, begin)
         when(72, 4 * CHUNKS, lambda i, c: compute_partial(c, facing(i)))
@@ -300,11 +374,23 @@
         for piece in range(4):
             once(112 + piece, functools.partial(relay, piece))
             once(116 + piece, functools.partial(landed, piece))
-        once(120, lambda: split_rows(0, r, 0, size))
-        once(121, lambda: split_rows(0, near, 0, size))
-        once(122, lambda: split_rows(1, r, 0, size))
-        once(123, lambda: split_rows(1, near, 0, size))
-
+        once(120, lambda: split_both(x_col, x_pair))
+        once(121, lambda: split_both(a_col, a_pair))
+        once(122, end_start)
+        once(123, end_middle)
+        once(126, end_last)
+        once(125, lambda: end_partials(CHUNKS - 1))
+
+    def split_both(source, pair_refs):
+        def one(i):
+            block = jnp.where(i == 0, r, near)
+            split_all(source.at[block], pair_refs, block)
+
+        loop(0, 2, one)
+
+    local[1].wait()
+    far_copy(0).start()
+    near_copy(0).start()
     local[0].wait()
 
     @pl.when(at_end)
@@ -315,9 +401,6 @@
     def _():
         loop(0, AHEAD, own_both)
 
-    local[1].wait()
-    far_copy(0).start()
-    near_copy(0).start()
     near_copy(1).start()
     near_wait(0)
     far_copy(1).start()
@@ -347,12 +430,14 @@
     def finish(c):
         update_ref[rows(c)] = update_ref[rows(c)] + partial[z, rows(c)]
 
-        @pl.when(z < last)
+        early = c < CHUNKS - LATE
+
+        @pl.when((z < last) & (early | (z != last - 1)))
         def _():
             reduce_wait(z, c)
             update_ref[rows(c)] = update_ref[rows(c)] + arrived[z, rows(c)]
 
-        @pl.when(z > 0)
+        @pl.when((z > 0) & (early | (z != 1)))
         def _():
             reduce_wait(n, c)
             update_ref[rows(c)] = update_ref[rows(c)] + arrived[n, rows(c)]
@@ -361,9 +446,11 @@
     loop(0, CHUNKS, finish)
 
     near_copy(1).wait_send()
-    for piece in range(2, 4):
-        far_copy(piece).wait_send()
-        relay_copy(piece).wait_send()
+
+    @pl.when(inside)
+    def _():
+        for which in range(3):
+            end_copy(which).wait_send()
 
     def sent(c):
         for hop in range(n - 1):
@@ -376,7 +463,7 @@
                 gather_pass(False, z + hop, c).wait_send()
 
         for d in range(n):
-            @pl.when(z != d)
+            @pl.when((z != d) & (inside | (c < CHUNKS - LATE) | (d == beside)))
             def _():
                 reduce_copy(z < d, d, c).wait_send()
 
@@ -414,6 +501,9 @@
             pltpu.SemaphoreType.DMA((n - 1, CHUNKS)),
             pltpu.SemaphoreType.DMA((n, CHUNKS)),
             pltpu.SemaphoreType.DMA((n + 1, CHUNKS)),
+            pltpu.SemaphoreType.DMA((3,)),
+            pltpu.SemaphoreType.DMA((3,)),
+            pltpu.SemaphoreType.REGULAR((2,)),
         ],
         compiler_params=pltpu.CompilerParams(
             collective_id=0, has_side_effects=True, vmem_limit_bytes=67043328

time: 226 us -> 220 us (0.973)
  Pallas kernels: 220 us -> 214 us
    pallas_call x1, Pallas kernels: 220 us -> 214 us  [per_device(): pl.pallas_call(functools.partial(kernel, n), out_shape=(shape, shape), in...]
where the time goes in v2:
time: 220 us; the launch traced here: 219 us
  Pallas kernels  214 us (97%)
  local copies, waits for them, and re-layouts  4.78 us (2%)
    pallas_call x1, Pallas kernels, per_device(): pl.pallas_call(functools.partial(kernel, n), out_shape=(shape, shape), in...  214 us
    unnamed x4, local copies, waits for them, and re-layouts  4.78 us

profile of v2, /device:TPU:0, one launch (start us, length us, event | category | flops | bytes accessed | tf_op | source)
XLA Modules:
  0.0 219.5 jit_solution(937369133152760914)
XLA Ops:
  0.6 214.1 %shard_map.41 = (f32[768,768]{1,0:T(8,128)}, f32[768,768]{1,0:T(8,128)}) custom-call(f32[768,768]{1,0:T(8,128)} %a_ref.1, f32[768,768]{1,0:T(8,128)} %x_ref.1), custom_call_target="tpu_custom_call" | custom-call | tf_op jit(solution)/shard_map/pallas_call | solution.py:477
  214.7 0.0 copy-start
  214.7 3.4 %copy.6 = f32[768,768]{1,0:T(8,128)} copy(f32[768,768]{1,0:T(8,128)} %get-tuple-element.4) | data formatting | bytes 4718592
  218.1 0.0 copy-done
  218.1 1.4 copy.7
Async XLA Ops:
  214.7 3.4 %copy-start = (f32[768,768]{1,0:T(8,128)S(1)}, f32[768,768]{1,0:T(8,128)}, u32[]{:S(2)}) copy-start(f32[768,768]{1,0:T(8,128)} %get-tuple-element.5) | copy-start | bytes 7077892

commit v3 on v2

--- a/solution.py
+++ b/solution.py
@@ -476,7 +476,7 @@
     shape = jax.ShapeDtypeStruct(transition.shape, f32)
     return pl.pallas_call(
         functools.partial(kernel, n),
-        out_shape=(shape, shape),
+        out_shape=(pltpu.VMEM(transition.shape, f32),) * 2,
         in_specs=[pl.BlockSpec(memory_space=pl.ANY)] * 2,
         out_specs=(pl.BlockSpec(memory_space=pltpu.VMEM),) * 2,
         scratch_shapes=[
@@ -506,7 +506,7 @@
             pltpu.SemaphoreType.REGULAR((2,)),
         ],
         compiler_params=pltpu.CompilerParams(
-            collective_id=0, has_side_effects=True, vmem_limit_bytes=67043328
+            collective_id=0, has_side_effects=True, vmem_limit_bytes=67043328 - 2 * 4 * transition.size
         ),
     )(transition, covariance)
 

time: 220 us -> 216 us (0.982)
    unnamed x4 -> x2, local copies, waits for them, and re-layouts: 4.78 us -> 2.81 us
where the time goes in v3:
time: 216 us; the launch traced here: 215 us
  Pallas kernels  212 us (98%)
  local copies, waits for them, and re-layouts  2.81 us (1%)
    pallas_call x1, Pallas kernels, per_device(): pl.pallas_call(functools.partial(kernel, n), out_shape=(pltpu.VMEM(transi...  212 us

profile of v3, /device:TPU:0, one launch (start us, length us, event | category | flops | bytes accessed | tf_op | source)
XLA Modules:
  0.0 215.4 jit_solution(1099786766537725652)
XLA Ops:
  0.6 211.9 %shard_map.41 = (f32[768,768]{1,0:T(8,128)S(1)}, f32[768,768]{1,0:T(8,128)S(1)}) custom-call(f32[768,768]{1,0:T(8,128)} %a_ref.1, f32[768,768]{1,0:T(8,128)} %x_ref.1), custom_call_target="tpu_custom_call" | custom-call | tf_op jit(solution)/shard_map/pallas_call | solution.py:477
  212.6 1.4 copy.6
  214.0 1.4 copy.7

commit v4 on v3

--- a/solution.py
+++ b/solution.py
@@ -12,26 +12,26 @@
 LATE = 1
 ORDERS = (
   (
-    255721738, 6686731, 38176921, 40303216, 8931872, 247220898, 152044195, 153457217,
-    13051202, 26289603, 240395799, 15296849, 207122550, 146345699, 174286565, 81095224,
-    64879033, 190209368, 196544347, 83469115, 181348190, 256648095, 32763879, 221911255,
-    225228072, 229439017, 233649962, 111877803, 258842413, 100630318,
+    33733880, 36061464, 245106970, 6834592, 8964642, 44497649, 24142912, 156279941,
+    158386980, 13052112, 173226308, 203262860, 79229281, 177533447, 119104157, 119761613,
+    256490483, 190209368, 196546395, 197370683, 181640806, 149411879, 167368927, 106572687,
+    108696681, 110826731, 129733997, 264952571, 95393391, 99456893,
   ),
   (
-    255721738, 6686731, 38176921, 40303216, 8931872, 247220898, 202375843, 136680024,
-    59813089, 141996294, 192465804, 15295090, 156394614, 210636491, 28403292, 163017392,
-    251452582, 171186334, 214861638, 175417182, 179640615, 149868502, 167244794, 219535759,
-    223286377, 227349739, 231691629, 93148655, 258693950, 100630318,
+    33733880, 36061464, 245106970, 6834592, 8964642, 44497649, 24522816, 204890245,
+    205886018, 13050330, 144485859, 152931212, 78832969, 160903687, 212950045, 100886237,
+    120175603, 173303930, 147754835, 103001958, 181758542, 105373095, 167244743, 219536911,
+    223138921, 227172075, 231560557, 265098747, 93020015, 99456893,
   ),
   (
-    245120248, 168835825, 154427592, 141732162, 248703474, 209236192, 242430532, 190213239,
-    212954715, 215066333, 219277150, 228259177, 177993581, 267758287, 268435455, 268435455,
+    245120248, 137378545, 173302096, 141731016, 248703474, 209236192, 242430532, 190213239,
+    162623067, 196699974, 221914086, 228046314, 234596973, 267757525, 268435455, 268435455,
     268435455, 268435455, 268435455, 268435455, 268435455, 268435455, 268435455, 268435455,
     268435455, 268435455, 268435455, 268435455, 268435455, 268435455,
   ),
   (
-    245120248, 202390257, 188244184, 141996354, 248967666, 158508232, 160903748, 212958195,
-    148121309, 171159398, 224031815, 175846866, 234174317, 267758287, 268435455, 268435455,
+    245120248, 185613041, 188244192, 141996354, 248967666, 158508232, 161033796, 146029555,
+    213165777, 175353542, 221914086, 228257642, 180074196, 267757551, 268435455, 268435455,
     268435455, 268435455, 268435455, 268435455, 268435455, 268435455, 268435455, 268435455,
     268435455, 268435455, 268435455, 268435455, 268435455, 268435455,
   ),
@@ -443,7 +443,7 @@
             update_ref[rows(c)] = update_ref[rows(c)] + arrived[n, rows(c)]
 
     local[2].wait()
-    loop(0, CHUNKS, finish)
+    loop(0, CHUNKS - 1, finish)
 
     near_copy(1).wait_send()
 
@@ -468,12 +468,12 @@
                 reduce_copy(z < d, d, c).wait_send()
 
     loop(0, CHUNKS, sent)
+    finish(CHUNKS - 1)
 
 
 def per_device(n, transition, covariance):
     size = transition.shape[0]
     f32, bf16 = jnp.float32, jnp.bfloat16
-    shape = jax.ShapeDtypeStruct(transition.shape, f32)
     return pl.pallas_call(
         functools.partial(kernel, n),
         out_shape=(pltpu.VMEM(transition.shape, f32),) * 2,

time: 216 us -> 214 us (level)
  no operation moved by 1% of the time
where the time goes in v4:
time: 214 us; the launch traced here: 213 us
  Pallas kernels  210 us (98%)
  local copies, waits for them, and re-layouts  2.81 us (1%)
    pallas_call x1, Pallas kernels, per_device(): pl.pallas_call(functools.partial(kernel, n), out_shape=(pltpu.VMEM(transi...  210 us

profile of v4, /device:TPU:0, one launch (start us, length us, event | category | flops | bytes accessed | tf_op | source)
XLA Modules:
  0.0 213.4 jit_solution(10176380537553679660)
XLA Ops:
  0.6 210.0 %shard_map.41 = (f32[768,768]{1,0:T(8,128)S(1)}, f32[768,768]{1,0:T(8,128)S(1)}) custom-call(f32[768,768]{1,0:T(8,128)} %a_ref.1, f32[768,768]{1,0:T(8,128)} %x_ref.1), custom_call_target="tpu_custom_call" | custom-call | tf_op jit(solution)/shard_map/pallas_call | solution.py:477
  210.6 1.4 copy.6
  212.0 1.4 copy.7

commit v5 on v4

--- a/solution.py
+++ b/solution.py
@@ -97,7 +97,7 @@
         pltpu.make_async_copy(x_ref, x_col.at[r], local_sems.at[1]),
         pltpu.make_async_copy(x_ref, update_ref, local_sems.at[2]),
     ]
-    for copy in local:
+    for copy in local[:2]:
         copy.start()
 
     barrier = pltpu.get_barrier_semaphore()
@@ -127,7 +127,7 @@
 
     def gather_own(right, c):
         landing, sems, to = gather_copy(right, z, c)
-        return remote(a_col.at[r, rows(c)], landing, *sems, col=to)
+        return remote(a_ref.at[rows(c)], landing, *sems, col=to)
 
     def gather_pass(right, block, c):
         landing, sems, to = gather_copy(right, block, c)
@@ -388,20 +388,20 @@
 
         loop(0, 2, one)
 
+    @pl.when(at_end)
+    def _():
+        loop(0, CHUNKS, own_both)
+
+    @pl.when(inside)
+    def _():
+        loop(0, AHEAD, own_both)
+
     local[1].wait()
     far_copy(0).start()
     near_copy(0).start()
     local[0].wait()
-
-    @pl.when(at_end)
-    def _():
-        loop(0, CHUNKS, own_both)
-
-    @pl.when(inside)
-    def _():
-        loop(0, AHEAD, own_both)
-
     near_copy(1).start()
+    local[2].start()
     near_wait(0)
     far_copy(1).start()
     near_wait(1)

time: 214 us -> 213 us (level)
  no operation moved by 1% of the time
where the time goes in v5:
time: 213 us
  Pallas kernels  209 us (98%)
  local copies, waits for them, and re-layouts  2.81 us (1%)
    pallas_call x1, Pallas kernels, per_device(): pl.pallas_call(functools.partial(kernel, n), out_shape=(pltpu.VMEM(transi...  209 us

profile of v5, /device:TPU:0, one launch (start us, length us, event | category | flops | bytes accessed | tf_op | source)
XLA Modules:
  0.0 212.6 jit_solution(11339234391024475535)
XLA Ops:
  0.6 209.2 %shard_map.41 = (f32[768,768]{1,0:T(8,128)S(1)}, f32[768,768]{1,0:T(8,128)S(1)}) custom-call(f32[768,768]{1,0:T(8,128)} %a_ref.1, f32[768,768]{1,0:T(8,128)} %x_ref.1), custom_call_target="tpu_custom_call" | custom-call | tf_op jit(solution)/shard_map/pallas_call | solution.py:477
  209.8 1.4 copy.6
  211.2 1.4 copy.7

commit v6 on v5

--- a/solution.py
+++ b/solution.py
@@ -471,10 +471,21 @@
     finish(CHUNKS - 1)
 
 
+def store(update_ref, square_ref, update_out, square_out, sems):
+    copies = [
+        pltpu.make_async_copy(update_ref, update_out, sems.at[0]),
+        pltpu.make_async_copy(square_ref, square_out, sems.at[1]),
+    ]
+    for copy in copies:
+        copy.start()
+    for copy in copies:
+        copy.wait()
+
+
 def per_device(n, transition, covariance):
     size = transition.shape[0]
     f32, bf16 = jnp.float32, jnp.bfloat16
-    return pl.pallas_call(
+    update, square = pl.pallas_call(
         functools.partial(kernel, n),
         out_shape=(pltpu.VMEM(transition.shape, f32),) * 2,
         in_specs=[pl.BlockSpec(memory_space=pl.ANY)] * 2,
@@ -509,6 +520,15 @@
             collective_id=0, has_side_effects=True, vmem_limit_bytes=67043328 - 2 * 4 * transition.size
         ),
     )(transition, covariance)
+    shape = jax.ShapeDtypeStruct(transition.shape, f32)
+    return pl.pallas_call(
+        store,
+        out_shape=(shape, shape),
+        in_specs=[pl.BlockSpec(memory_space=pl.ANY)] * 2,
+        out_specs=(pl.BlockSpec(memory_space=pl.ANY),) * 2,
+        scratch_shapes=[pltpu.SemaphoreType.DMA((2,))],
+        compiler_params=pltpu.CompilerParams(vmem_limit_bytes=1 << 20),
+    )(update, square)
 
 
 def solution(mesh):

time: 213 us -> 212 us (level)
  local copies, waits for them, and re-layouts: 2.81 us -> 0 us
    unnamed x2 -> x0, local copies, waits for them, and re-layouts: 2.81 us -> none
    pallas_call x0 -> x1, Pallas kernels: none -> 2.2 us  [per_device(): pl.pallas_call(store, out_shape=(shape, shape), in_specs=[pl.BlockSpec(me...]
where the time goes in v6:
time: 212 us
  Pallas kernels  211 us (100%)
    pallas_call x1, Pallas kernels, per_device(): pl.pallas_call(functools.partial(kernel, n), out_shape=(pltpu.VMEM(transi...  209 us

profile of v6, /device:TPU:0, one launch (start us, length us, event | category | flops | bytes accessed | tf_op | source)
XLA Modules:
  0.0 212.0 jit_solution(10420011049857520096)
XLA Ops:
  0.6 209.2 %shard_map.41 = (f32[768,768]{1,0:T(8,128)S(1)}, f32[768,768]{1,0:T(8,128)S(1)}) custom-call(f32[768,768]{1,0:T(8,128)} %a_ref.1, f32[768,768]{1,0:T(8,128)} %x_ref.1), custom_call_target="tpu_custom_call" | custom-call | tf_op jit(solution)/shard_map/pallas_call | solution.py:488
  209.8 2.2 %shard_map.42 = (f32[768,768]{1,0:T(8,128)}, f32[768,768]{1,0:T(8,128)}) custom-call(f32[768,768]{1,0:T(8,128)S(1)} %get-tuple-element.4.update_ref, f32[768,768]{1,0:T(8,128)S(1)} %get-tuple-element.5.square_ref), custom_call_target="tpu_custom_call" | custom-call | tf_op jit(solution)/shard_map/pallas_call | solution.py:524
